TPU v7x, 32 devices: a whole 2x2x4 slice. The times are simulated.
32 devices in a mesh: group: 2 (over y), seq: 4 (over z), tensor: 4 (over x, core).
Axes of the slice: x: 2, y: 2, z: 4, core: 2. Of those that a mesh axis runs over, the one named last changes fastest.
Arguments:
- query: bfloat16 [16, 7168], P(('group', 'seq'), 'tensor'), parts along dimension 0, may hold values from -5 to 5
- key_cache: bfloat16 [32, 256, 7168], P(('group', 'seq'), None, 'tensor'), parts along dimension 0, may hold values from -5 to 5
- value_cache: bfloat16 [32, 256, 7168], P(('group', 'seq'), None, 'tensor'), parts along dimension 0, may hold values from -6 to 6
- alibi_slopes: float32 [56], P('tensor'), may hold values from 0 to 1, as said below
- block_seq: int32 [32], P(('group', 'seq')), parts along dimension 0, may hold values from 0 to 7, as said below
- block_pos: int32 [32], P(('group', 'seq')), parts along dimension 0, may hold values from 0 to 2, as said below
- lengths: int32 [16], P('group'), parts along dimension 0, may hold values from 1 to 768, as said below
- out_weight: bfloat16 [7168, 14336], P('tensor', 'seq'), may hold values from -0.5 to 0.5
Outputs:
- mixed: bfloat16 [16, 14336], P(('group', 'tensor'), 'seq'), parts along dimension 0
There are 2 independent parts, one for each index of `group`. A program takes and returns all parts, laid end to end along the dimension named above; an argument that names none is the same for every part. Nothing has to cross between parts.
Inputs may be any that keep to these rules, and one draw needn't show every extreme that they name: `block_seq`: every sequence owns at least one block and at most 3; the blocks of sequence s have block_pos 0 to n_s - 1, each once. block_pos of a block is below the number of blocks its sequence owns. `lengths`: A sequence that owns n blocks has a length above 256 * (n - 1) and at most 256 * n. `alibi_slopes`: positive slopes.
All inputs are finite; a program needn't handle non-finite values.
Results may differ from a plain program's by a relative error of at most 0.0054.
Values may be sent and summed in bfloat16 or wider, within the bound.
A program may use at most 64 MiB of HBM per device.

v0:
```python
import math

import jax
import jax.numpy as jnp
from jax import lax
from jax.sharding import PartitionSpec as P


def local(query, key_cache, value_cache, alibi_slopes, block_seq, block_pos, lengths, out_weight):
    heads = alibi_slopes.shape[0]
    features = query.shape[1]
    head_size = features // heads
    blocks_here = key_cache.shape[0]
    block_len = key_cache.shape[1]
    seq_count = lengths.shape[0]
    scale = 1.0 / math.sqrt(head_size)
    whole_query = lax.all_gather(query, "seq", axis=0, tiled=True)
    query_rows = jnp.take(whole_query, block_seq, axis=0).reshape(blocks_here, heads, head_size)
    keys = key_cache.reshape(blocks_here, block_len, heads, head_size)
    values = value_cache.reshape(blocks_here, block_len, heads, head_size)
    scores = (
        jnp.einsum("bthd,bhd->bht", keys, query_rows, preferred_element_type=jnp.float32) * scale
    )
    owner_length = lengths[block_seq]
    placed = block_pos[:, None] * block_len + jnp.arange(block_len, dtype=jnp.int32)[None, :]
    live = (placed < owner_length[:, None])[:, None, :]
    distance = (owner_length[:, None] - 1 - placed).astype(jnp.float32)
    scores = scores - alibi_slopes[None, :, None] * distance[:, None, :]
    scores = jnp.where(live, scores, -1e30)
    block_top = jnp.max(scores, axis=2)
    weights = jnp.where(live, jnp.exp(scores - block_top[:, :, None]), 0.0)
    block_total = jnp.sum(weights, axis=2)
    block_acc = jnp.einsum(
        "bht,bthd->bhd", weights.astype(jnp.bfloat16), values, preferred_element_type=jnp.float32
    )
    seq_ids = jnp.arange(seq_count, dtype=jnp.int32)
    owned = (block_seq[None, :] == seq_ids[:, None])[:, :, None]
    local_top = jnp.max(jnp.where(owned, block_top[None], -1e30), axis=1)
    factor = jnp.where(owned, jnp.exp(block_top[None] - local_top[:, None, :]), 0.0)
    local_total = jnp.sum(factor * block_total[None], axis=1)
    local_acc = jnp.einsum("sbh,bhd->shd", factor, block_acc, precision=lax.Precision.HIGHEST)
    tops, totals, accs = (
        lax.all_to_all(local_top[None], "seq", split_axis=1, concat_axis=0, tiled=True),
        lax.all_to_all(local_total[None], "seq", split_axis=1, concat_axis=0, tiled=True),
        lax.all_to_all(local_acc[None], "seq", split_axis=1, concat_axis=0, tiled=True),
    )
    best = jnp.max(tops, axis=0)
    scaling = jnp.exp(tops - best[None])
    home_total = jnp.sum(totals * scaling, axis=0)
    home_acc = jnp.sum(accs * scaling[..., None], axis=0)
    mine = (
        (home_acc / home_total[:, :, None])
        .astype(jnp.bfloat16)
        .reshape(home_acc.shape[0], features)
    )
    attention = lax.all_gather(mine, "seq", axis=0, tiled=True)
    mixed = lax.psum_scatter(
        jnp.dot(attention, out_weight, preferred_element_type=jnp.float32),
        "tensor",
        scatter_dimension=0,
        tiled=True,
    )
    return mixed.astype(jnp.bfloat16)


def solution(mesh):
    placed = (
        P(("group", "seq"), "tensor"),
        P(("group", "seq"), None, "tensor"),
        P(("group", "seq"), None, "tensor"),
        P("tensor"),
        P(("group", "seq")),
        P(("group", "seq")),
        P("group"),
        P("tensor", "seq"),
    )
    return jax.shard_map(
        local, mesh=mesh, in_specs=placed, out_specs=P(("group", "tensor"), "seq"), check_vma=False
    )
```

profile of v0, /device:TPU:0, one launch (start us, length us, event | category | flops | bytes accessed | tf_op | source)
XLA Modules:
  0.0 95.4 jit_solution(14486349411866468453)
XLA Ops:
  0.0 0.0 copy-start
  0.0 0.7 compare_select_fusion
  0.7 0.7 compare_and_fusion
  1.3 0.7 iota_compare_fusion
  2.1 0.0 copy-done
  2.1 0.6 gather_fusion
  2.7 0.7 broadcast_add_fusion
  3.4 0.1 fusion.16
  3.5 0.1 subtract_convert_fusion
  3.5 15.1 %all-gather = bf16[4,2,1792]{2,1,0:T(2,128)(2,1)S(1)} all-gather(bf16[1,2,1792]{2,1,0:T(2,128)(2,1)} %bitcast.41), channel_id=1, replica_groups=mesh['group'=2,'seq'=4,'tensor'=4] {'seq'}, dimensions={0}, use_global_device_ids=true | all-gather | bytes 35840 | tf_op jit(solution)/shard_map/all_gather | solution.py:17
  18.6 0.6 gather_fusion.1
  19.2 6.0 %copy.49 = bf16[4,256,1792]{1,2,0:T(8,128)(2,1)} copy(bf16[4,256,1792]{2,1,0:T(8,128)(2,1)} %param.9) | data formatting | bytes 7340032 | tf_op args[1]
  25.2 0.0 copy-start.1
  25.2 0.1 select_bitcast_fusion
  25.3 2.6 %fusion.9 = f32[4,14,1,256]{3,2,1,0:T(1,128)S(1)} fusion(bf16[4,256,14,128]{1,3,2,0:T(8,128)(2,1)} %bitcast.33, bf16[4,14,128,1]{2,1,0,3:T(8,128)(2,1)S(1)} %select_bitcast_fusion), kind=kOutput, calls=%fused_computation.16 | convolution fusion | flops 3670016 | bytes 3741696 | tf_op jit(solution)/shard_map/bthd,bhd->bht/dot_general | solution.py:22
  27.9 0.0 copy-done.1
  27.9 0.2 fusion.18
  28.0 0.1 select_reduce_fusion
  28.1 0.7 copy.54
  28.8 4.7 %all-to-all-start.1 = ((f32[1,8,14]{2,0,1:T(1,128)}), f32[1,8,14]{2,0,1:T(1,128)S(1)}, u32[]{:S(2)}, u32[]{:S(2)}) async-start(f32[1,8,14]{2,0,1:T(1,128)} %copy.54), calls=%async_computation.1 | async-start | bytes 8192 | tf_op jit(solution)/shard_map/all_to_all | solution.py:43
  33.6 0.2 fusion.4
  33.7 0.1 multiply_reduce_fusion.1
  33.8 6.0 %copy.50 = bf16[4,256,1792]{1,2,0:T(8,128)(2,1)} copy(bf16[4,256,1792]{2,1,0:T(8,128)(2,1)} %param.10) | data formatting | bytes 7340032 | tf_op args[2]
  39.8 0.0 copy-start.2
  39.8 3.1 %fusion.2 = f32[4,14,1,128]{3,2,1,0:T(1,128)S(1)} fusion(bf16[4,256,14,128]{1,3,2,0:T(8,128)(2,1)} %bitcast.34, bf16[4,14,256,1]{2,0,1,3:T(4,128)(2,1)S(1)} %get-tuple-element.10), kind=kOutput, calls=%fused_computation.6 | convolution fusion | flops 3670016 | bytes 3727360 | tf_op jit(solution)/shard_map/bht,bthd->bhd/dot_general | solution.py:33
  42.9 0.4 convolution_bitcast_fusion
  43.3 0.7 copy.57
  44.0 0.0 all-to-all-done.1
  44.0 5.1 %all-to-all-start.2 = ((f32[1,8,14]{2,0,1:T(1,128)}), f32[1,8,14]{2,0,1:T(1,128)S(1)}, u32[]{:S(2)}, u32[]{:S(2)}) async-start(f32[1,8,14]{2,0,1:T(1,128)} %copy.57), calls=%async_computation.2 | async-start | bytes 8192 | tf_op jit(solution)/shard_map/all_to_all | solution.py:44
  49.1 0.7 copy.51
  49.7 0.0 copy-done.2
  49.7 0.6 dynamic-slice
  51.0 3.7 %all-to-all-done.2 = f32[1,8,14]{2,0,1:T(1,128)S(1)} async-done(((f32[1,8,14]{2,0,1:T(1,128)}), f32[1,8,14]{2,0,1:T(1,128)S(1)}, u32[]{:S(2)}, u32[]{:S(2)}) %all-to-all-start.2) | async-done | bytes 480 | tf_op jit(solution)/shard_map/all_to_all | solution.py:44
  54.6 3.3 %all-to-all-start = ((f32[1,8,14,128]{3,0,2,1:T(1,128)}), f32[1,8,14,128]{3,0,2,1:T(1,128)S(1)}, u32[]{:S(2)}, u32[]{:S(2)}) async-start(f32[1,8,14,128]{3,0,2,1:T(1,128)} %copy.51), calls=%async_computation | async-start | bytes 114688 | tf_op jit(solution)/shard_map/all_to_all | solution.py:45
  58.0 0.1 copy.55
  58.1 0.1 copy.58
  58.2 5.5 %all-to-all-done = f32[1,8,14,128]{3,0,2,1:T(1,128)S(1)} async-done(((f32[1,8,14,128]{3,0,2,1:T(1,128)}), f32[1,8,14,128]{3,0,2,1:T(1,128)S(1)}, u32[]{:S(2)}, u32[]{:S(2)}) %all-to-all-start) | async-done | bytes 57376 | tf_op jit(solution)/shard_map/all_to_all | solution.py:45
  63.6 0.1 multiply_reduce_fusion
  63.8 0.1 fusion.15
  63.9 13.2 %all-gather.1 = bf16[4,2,1792]{2,1,0:T(2,128)(2,1)S(1)} all-gather(bf16[1,2,1792]{2,1,0:T(2,128)(2,1)S(1)} %fusion.15), channel_id=1, replica_groups=mesh['group'=2,'seq'=4,'tensor'=4] {'seq'}, dimensions={0}, use_global_device_ids=true | all-gather | bytes 35840 | tf_op jit(solution)/shard_map/all_gather | solution.py:56
  77.1 6.4 %fusion.20 = f32[8,3584]{1,0:T(8,128)S(1)} fusion(bf16[8,1792]{1,0:T(8,128)(2,1)S(1)} %reshape.152, bf16[1792,3584]{1,0:T(8,128)(2,1)} %param.15), kind=kOutput, calls=%fused_computation.41 | convolution fusion | flops 102760448 | bytes 12988416 | tf_op jit(solution)/shard_map/dot_general | solution.py:58
  83.5 11.3 %all-reduce = bf16[8,3584]{1,0:T(8,128)(2,1)S(1)} all-reduce(f32[8,3584]{1,0:T(8,128)S(1)} %fusion.20), channel_id=2, replica_groups=mesh['group'=2,'seq'=4,'tensor'=4] {'tensor'}, use_global_device_ids=true, to_apply=%region_7.8.clone | all-reduce | flops 28672 | bytes 172032
  94.7 0.6 dynamic-slice_convert_fusion
  (7 shorter events, 0.1 us)
Async XLA Ops:
  0.0 2.1 %copy-start = (s32[8]{0:T(128)S(1)}, s32[8]{0:T(128)}, u32[]{:S(2)}) copy-start(s32[8]{0:T(128)} %param.14) | copy-start | bytes 100
  25.2 2.7 %copy-start.1 = (f32[14]{0:T(128)S(1)}, f32[14]{0:T(128)}, u32[]{:S(2)}) copy-start(f32[14]{0:T(128)} %param.11) | copy-start | bytes 172
  28.8 15.2 %all-to-all-start.1 = ((f32[1,8,14]{2,0,1:T(1,128)}), f32[1,8,14]{2,0,1:T(1,128)S(1)}, u32[]{:S(2)}, u32[]{:S(2)}) async-start(f32[1,8,14]{2,0,1:T(1,128)} %copy.54), calls=%async_computation.1 | async-start | bytes 8192 | tf_op jit(solution)/shard_map/all_to_all | solution.py:43
  39.8 9.9 %copy-start.2 = (u32[32]{0:T(128)S(1)}, u32[32]{0:T(128)}, u32[]{:S(2)}) copy-start(u32[32]{0:T(128)} %constant.39) | copy-start | bytes 388
  44.0 10.7 %all-to-all-start.2 = ((f32[1,8,14]{2,0,1:T(1,128)}), f32[1,8,14]{2,0,1:T(1,128)S(1)}, u32[]{:S(2)}, u32[]{:S(2)}) async-start(f32[1,8,14]{2,0,1:T(1,128)} %copy.57), calls=%async_computation.2 | async-start | bytes 8192 | tf_op jit(solution)/shard_map/all_to_all | solution.py:44
  54.6 9.0 %all-to-all-start = ((f32[1,8,14,128]{3,0,2,1:T(1,128)}), f32[1,8,14,128]{3,0,2,1:T(1,128)S(1)}, u32[]{:S(2)}, u32[]{:S(2)}) async-start(f32[1,8,14,128]{3,0,2,1:T(1,128)} %copy.51), calls=%async_computation | async-start | bytes 114688 | tf_op jit(solution)/shard_map/all_to_all | solution.py:45
where the time goes:
time: 96.1 us; the launch traced here: 95.4 us
  blocking collectives  39.5 us (41%)
  local copies, waits for them, and re-layouts  16.7 us (17%)
  starting transfers between devices  13.1 us (14%)
  matrix products  12.5 us (13%)
  waiting for transfers between devices  9.12 us (9%)
  other arithmetic  3.75 us (4%)
    all_gather x1, blocking collectives, local(): whole_query = lax.all_gather(query, 'seq', axis=0, tiled=True)  15.1 us
    all_gather x1, blocking collectives, local(): attention = lax.all_gather(mine, 'seq', axis=0, tiled=True)  13.2 us
    unnamed x11, local copies, waits for them, and re-layouts  12.6 us
    unnamed x1, blocking collectives  11.3 us
    dot_general x1, matrix products, local(): jnp.dot(attention, out_weight, preferred_element_type=jnp.float32)  6.41 us
    all_to_all x1, waiting for transfers between devices, local(): lax.all_to_all(local_acc[None], 'seq', split_axis=1, concat_axis=0, tiled...  5.46 us
    all_to_all x1, starting transfers between devices, local(): lax.all_to_all(local_total[None], 'seq', split_axis=1, concat_axis=0, til...  5.09 us
    all_to_all x1, starting transfers between devices, local(): lax.all_to_all(local_top[None], 'seq', split_axis=1, concat_axis=0, tiled...  4.74 us
  transfers between devices with their start and end apart: 3, of which 2 were waited for; matrix products, arithmetic and copies ran while one was open for 13% of the time, Pallas kernels for 0%

commit v1 on v0

v1 whole, which is shorter than its diff:
```python
import functools
import math

import jax
import jax.numpy as jnp
from jax import lax
from jax.experimental import pallas as pl
from jax.experimental.pallas import tpu as pltpu
from jax.sharding import PartitionSpec as P

LANES = 128
OWNER_LANE = LANES - 1


def kernel(
    seq_size, tensor_size, heads, chunks,
    block_seq, block_pos, lengths, slopes, query, keys, values, weight,
    out,
    q_all, k_buf, v_buf, w_buf, stats, accs, part, landed,
    q_sem, k_sem, v_sem, w_sem,
    q_send, q_recv, s_send, s_recv, a_send, a_recv, p_send, p_recv,
):
    me = lax.axis_index("seq")
    my_rows = lax.axis_index("tensor")
    blocks, block_len, features = k_buf.shape
    size = features // heads
    padded = -(-heads // 16) * 16
    seqs = lengths.shape[0]
    query_rows = q_all.shape[1]
    rows, width = part.shape[2:]
    scale = 1.0 / math.sqrt(size)

    q_copy = pltpu.make_async_copy(query, q_all.at[me], q_sem)
    q_copy.start()
    k_copies = [
        pltpu.make_async_copy(keys.at[b], k_buf.at[b], k_sem.at[b]) for b in range(blocks)
    ]
    v_copies = [
        pltpu.make_async_copy(values.at[b], v_buf.at[b], v_sem.at[b]) for b in range(blocks)
    ]
    w_copies = [
        pltpu.make_async_copy(
            weight.at[:, pl.ds(c * width, width)],
            w_buf.at[:, pl.ds(c * width, width)],
            w_sem.at[c],
        )
        for c in range(chunks)
    ]
    for copy in k_copies + v_copies + w_copies:
        copy.start()

    barrier = pltpu.get_barrier_semaphore()
    for k in range(1, seq_size):
        pl.semaphore_signal(barrier, inc=1, device_id={"seq": lax.rem(me + k, seq_size)})
    for k in range(1, tensor_size):
        pl.semaphore_signal(
            barrier, inc=1, device_id={"tensor": lax.rem(my_rows + k, tensor_size)}
        )
    pl.semaphore_wait(barrier, seq_size + tensor_size - 2)

    def to_seq(buffer, send, recv):
        copies = [
            pltpu.make_async_remote_copy(
                src_ref=buffer.at[me],
                dst_ref=buffer.at[me],
                send_sem=send.at[k - 1],
                recv_sem=recv.at[k - 1],
                device_id={"seq": lax.rem(me + k, seq_size)},
            )
            for k in range(1, seq_size)
        ]
        for copy in copies:
            copy.start()
        return copies

    q_copy.wait()
    q_sends = to_seq(q_all, q_send, q_recv)

    lane = lax.broadcasted_iota(jnp.int32, (padded, features), 1)
    row = lax.broadcasted_iota(jnp.int32, (padded, features), 0)
    of_head = (lane >= row * size) & (lane < row * size + size)
    head_row = lax.broadcasted_iota(jnp.int32, (padded, LANES), 0)
    head_lane = lax.broadcasted_iota(jnp.int32, (padded, LANES), 1)
    slope = jnp.zeros((padded, LANES), jnp.float32)
    for h in range(heads):
        slope = jnp.where(head_row == h, slopes[h], slope)
    slope = slope[:, :1]
    offsets = lax.broadcasted_iota(jnp.int32, (1, block_len), 1)
    stat_lane = lax.broadcasted_iota(jnp.int32, (1, LANES), 1)

    for copy in q_sends:
        copy.wait_recv()

    weights, inverse, stat_rows = [], [], []
    for b in range(blocks):
        owner = block_seq[b]
        length = lengths[owner]
        near = q_all[lax.div(owner, query_rows)].astype(jnp.float32)
        which = lax.rem(owner, query_rows)
        q_row = near[:1]
        for r in range(1, query_rows):
            q_row = jnp.where(which == r, near[r : r + 1], q_row)
        spread = jnp.where(of_head, q_row, 0.0).astype(jnp.bfloat16)
        k_copies[b].wait()
        scores = lax.dot_general(
            spread, k_buf[b], (((1,), (1,)), ((), ())), preferred_element_type=jnp.float32
        )
        placed = block_pos[b] * block_len + offsets
        live = placed < length
        distance = (length - 1 - placed).astype(jnp.float32)
        scores = jnp.where(live, scores * scale - slope * distance, -1e30)
        top = jnp.max(scores, axis=1, keepdims=True)
        weight_b = jnp.where(live, jnp.exp(scores - top), 0.0)
        total = jnp.sum(weight_b, axis=1, keepdims=True)
        weights.append(weight_b.astype(jnp.bfloat16))
        inverse.append(1.0 / total)
        stat = jnp.sum(
            jnp.where(head_row == head_lane, top + jnp.log(total), 0.0), axis=0, keepdims=True
        )
        stat_rows.append(jnp.where(stat_lane == OWNER_LANE, owner.astype(jnp.float32), stat))
    stats[me] = jnp.concatenate(stat_rows, axis=0)
    s_sends = to_seq(stats, s_send, s_recv)

    acc_rows = []
    for b in range(blocks):
        v_copies[b].wait()
        summed = jnp.dot(weights[b], v_buf[b], preferred_element_type=jnp.float32)
        summed = summed * inverse[b]
        acc_rows.append(
            jnp.sum(jnp.where(of_head, summed, 0.0), axis=0, keepdims=True)
        )
    accs[me] = jnp.concatenate(acc_rows, axis=0).astype(jnp.bfloat16)
    a_sends = to_seq(accs, a_send, a_recv)

    for copy in s_sends:
        copy.wait_recv()
    stat = stats[...]
    owners = stat[:, :, OWNER_LANE:]
    best = jnp.zeros_like(stat)
    masks = [owners == float(s) for s in range(seqs)]
    for s in range(seqs):
        top = jnp.max(jnp.where(masks[s], stat, -1e30), axis=(0, 1), keepdims=True)
        best = jnp.where(masks[s], top, best)
    grown = jnp.exp(stat - best)
    whole = jnp.ones_like(stat)
    for s in range(seqs):
        total = jnp.sum(jnp.where(masks[s], grown, 0.0), axis=(0, 1), keepdims=True)
        whole = jnp.where(masks[s], total, whole)
    factor = grown / whole
    seq_lane = lax.broadcasted_iota(jnp.int32, (blocks, LANES), 1).astype(jnp.float32)
    owned = jnp.concatenate(
        [jnp.where(owners[j] == seq_lane, 1.0, 0.0) for j in range(seq_size)], axis=0
    )
    owned = owned.T[:seqs].astype(jnp.bfloat16)
    spread = [
        jnp.concatenate(
            [jnp.broadcast_to(factor[j][:, h : h + 1], (blocks, size)) for h in range(heads)],
            axis=1,
        )
        for j in range(seq_size)
    ]

    for copy in a_sends:
        copy.wait_recv()
    scaled = jnp.concatenate(
        [accs[j].astype(jnp.float32) * spread[j] for j in range(seq_size)], axis=0
    )
    high = scaled.astype(jnp.bfloat16)
    low = (scaled - high.astype(jnp.float32)).astype(jnp.bfloat16)
    attention = jnp.dot(owned, high, preferred_element_type=jnp.float32) + jnp.dot(
        owned, low, preferred_element_type=jnp.float32
    )
    attention = attention.astype(jnp.bfloat16)

    p_sends = []
    for c in range(chunks):
        w_copies[c].wait()
        product = jnp.dot(
            attention, w_buf[:, c * width : (c + 1) * width], preferred_element_type=jnp.float32
        )
        for r in range(tensor_size):
            part[r, c] = product[r * rows : (r + 1) * rows]
        sends = []
        for k in range(1, tensor_size):
            peer = lax.rem(my_rows + k, tensor_size)
            copy = pltpu.make_async_remote_copy(
                src_ref=part.at[peer, c],
                dst_ref=landed.at[k - 1, c],
                send_sem=p_send.at[k - 1, c],
                recv_sem=p_recv.at[k - 1, c],
                device_id={"tensor": peer},
            )
            copy.start()
            sends.append(copy)
        p_sends.append(sends)
    for c in range(chunks):
        total = part[my_rows, c]
        for k in range(1, tensor_size):
            p_sends[c][k - 1].wait_recv()
            total = total + landed[k - 1, c]
        out[:, c * width : (c + 1) * width] = total.astype(out.dtype)
    for copy in q_sends + s_sends + a_sends + [copy for sends in p_sends for copy in sends]:
        copy.wait_send()


def local(seq_size, tensor_size, query, key_cache, value_cache, slopes, block_seq, block_pos, lengths, weight):
    heads = slopes.shape[0]
    blocks, block_len, features = key_cache.shape
    columns = weight.shape[1]
    chunks = max([c for c in range(1, 9) if columns % (c * 256) == 0], default=1)
    width = columns // chunks
    rows = lengths.shape[0] // tensor_size
    smem = pl.BlockSpec(memory_space=pltpu.SMEM)
    anywhere = pl.BlockSpec(memory_space=pl.ANY)
    dma = pltpu.SemaphoreType.DMA
    return pl.pallas_call(
        functools.partial(kernel, seq_size, tensor_size, heads, chunks),
        out_shape=jax.ShapeDtypeStruct((rows, columns), jnp.bfloat16),
        in_specs=[smem] * 4 + [anywhere] * 4,
        out_specs=pl.BlockSpec(memory_space=pltpu.VMEM),
        scratch_shapes=[
            pltpu.VMEM((seq_size,) + query.shape, query.dtype),
            pltpu.VMEM(key_cache.shape, key_cache.dtype),
            pltpu.VMEM(value_cache.shape, value_cache.dtype),
            pltpu.VMEM(weight.shape, weight.dtype),
            pltpu.VMEM((seq_size, blocks, LANES), jnp.float32),
            pltpu.VMEM((seq_size, blocks, features), jnp.bfloat16),
            pltpu.VMEM((tensor_size, chunks, rows, width), jnp.float32),
            pltpu.VMEM((tensor_size - 1, chunks, rows, width), jnp.float32),
            dma,
            dma((blocks,)),
            dma((blocks,)),
            dma((chunks,)),
        ]
        + [dma((seq_size - 1,))] * 6
        + [dma((tensor_size - 1, chunks))] * 2,
        compiler_params=pltpu.CompilerParams(collective_id=0, has_side_effects=True),
    )(block_seq, block_pos, lengths, slopes, query, key_cache, value_cache, weight)


def solution(mesh):
    placed = (
        P(("group", "seq"), "tensor"),
        P(("group", "seq"), None, "tensor"),
        P(("group", "seq"), None, "tensor"),
        P("tensor"),
        P(("group", "seq")),
        P(("group", "seq")),
        P("group"),
        P("tensor", "seq"),
    )
    return jax.shard_map(
        functools.partial(local, mesh.shape["seq"], mesh.shape["tensor"]),
        mesh=mesh,
        in_specs=placed,
        out_specs=P(("group", "tensor"), "seq"),
        check_vma=False,
    )
```

time: 96.1 us -> 28.6 us (0.30)
  blocking collectives: 39.5 us -> 0 us
  Pallas kernels: 0 us -> 27 us
  local copies, waits for them, and re-layouts: 16.7 us -> 1.32 us
  starting transfers between devices: 13.1 us -> 0 us
  matrix products: 12.5 us -> 0 us
  waiting for transfers between devices: 9.12 us -> 0 us
  other arithmetic: 3.75 us -> 0 us
    all_gather x2 -> x0, blocking collectives: 28.2 us -> none  [the longest x1 15.1 us: local(): whole_query = lax.all_gather(query, 'seq', axis=0, tiled=True)]
    pallas_call x0 -> x1, Pallas kernels: none -> 27 us  [local(): pl.pallas_call(functools.partial(kernel, seq_size, tensor_size, heads, ch...]
    all_to_all x3 -> x0, starting transfers between devices: 13.1 us -> none  [the longest x1 5.09 us: local(): lax.all_to_all(local_total[None], 'seq', split_axis=1, concat_axis=0, til...]
    dot_general x4 -> x0, matrix products: 12.5 us -> none  [the longest x1 6.41 us: local(): jnp.dot(attention, out_weight, preferred_element_type=jnp.float32)]
    unnamed x1 -> x0, blocking collectives: 11.3 us -> none
    unnamed x11 -> x1, local copies, waits for them, and re-layouts: 12.6 us -> 1.32 us
    all_to_all x3 -> x0, waiting for transfers between devices: 9.12 us -> none  [the longest x1 5.46 us: local(): lax.all_to_all(local_acc[None], 'seq', split_axis=1, concat_axis=0, tiled...]
    broadcast_in_dim x3 -> x0, local copies, waits for them, and re-layouts: 2.02 us -> none  [the longest x1 0.68 us: local(): local_acc[None]]
  transfers between devices with their start and end apart: 3 -> 0, of which waited for: 2 -> 0; matrix products, arithmetic and copies ran while one was open for 13% -> 0% of each run, Pallas kernels for 0% -> 0%
where the time goes in v1:
time: 28.6 us; the launch traced here: 28.4 us
  Pallas kernels  27 us (94%)
  local copies, waits for them, and re-layouts  1.32 us (5%)
    pallas_call x1, Pallas kernels, local(): pl.pallas_call(functools.partial(kernel, seq_size, tensor_size, heads, ch...  27 us
    unnamed x1, local copies, waits for them, and re-layouts  1.32 us

profile of v1, /device:TPU:0, one launch (start us, length us, event | category | flops | bytes accessed | tf_op | source)
XLA Modules:
  0.0 28.4 jit_solution(11320518578730904074)
XLA Ops:
  0.0 27.0 %shard_map.82 = bf16[2,3584]{1,0:T(2,128)(2,1)} custom-call(s32[4]{0:T(128)} %block_seq.1, s32[4]{0:T(128)} %block_pos.1, s32[8]{0:T(128)} %lengths.1, f32[14]{0:T(128)} %slopes.1, bf16[2,1792]{1,0:T(2,128)(2,1)} %query.1, bf16[4,256,1792]{2,1,0:T(8,128)(2,1)} %keys.1, bf16[4,256,1792]{2,1,0:T(8,128)(2,1)} %values.1, bf16[1792,3584]{1,0:T(8,128)(2,1)} %weight.1), custom_call_target="tpu_custom_call" | custom-call | tf_op jit(solution)/shard_map/pallas_call | solution.py:216
  27.0 1.3 %copy.10 = bf16[2,3584]{1,0:T(2,128)(2,1)} copy(bf16[2,3584]{1,0:T(2,128)(2,1)} %shard_map.82) | data formatting | bytes 28672

commit v2 on v1

--- a/solution.py
+++ b/solution.py
@@ -46,9 +46,6 @@
         )
         for c in range(chunks)
     ]
-    for copy in k_copies + v_copies + w_copies:
-        copy.start()
-
     barrier = pltpu.get_barrier_semaphore()
     for k in range(1, seq_size):
         pl.semaphore_signal(barrier, inc=1, device_id={"seq": lax.rem(me + k, seq_size)})
@@ -56,6 +53,9 @@
         pl.semaphore_signal(
             barrier, inc=1, device_id={"tensor": lax.rem(my_rows + k, tensor_size)}
         )
+    q_copy.wait()
+    for copy in k_copies + v_copies:
+        copy.start()
     pl.semaphore_wait(barrier, seq_size + tensor_size - 2)
 
     def to_seq(buffer, send, recv):
@@ -73,7 +73,6 @@
             copy.start()
         return copies
 
-    q_copy.wait()
     q_sends = to_seq(q_all, q_send, q_recv)
 
     lane = lax.broadcasted_iota(jnp.int32, (padded, features), 1)
@@ -90,6 +89,10 @@
 
     for copy in q_sends:
         copy.wait_recv()
+    for copy in w_copies:
+        copy.start()
+    for copy in k_copies + v_copies:
+        copy.wait()
 
     weights, inverse, stat_rows = [], [], []
     for b in range(blocks):
@@ -101,7 +104,6 @@
         for r in range(1, query_rows):
             q_row = jnp.where(which == r, near[r : r + 1], q_row)
         spread = jnp.where(of_head, q_row, 0.0).astype(jnp.bfloat16)
-        k_copies[b].wait()
         scores = lax.dot_general(
             spread, k_buf[b], (((1,), (1,)), ((), ())), preferred_element_type=jnp.float32
         )
@@ -123,7 +125,6 @@
 
     acc_rows = []
     for b in range(blocks):
-        v_copies[b].wait()
         summed = jnp.dot(weights[b], v_buf[b], preferred_element_type=jnp.float32)
         summed = summed * inverse[b]
         acc_rows.append(
@@ -173,8 +174,9 @@
     attention = attention.astype(jnp.bfloat16)
 
     p_sends = []
+    for copy in w_copies:
+        copy.wait()
     for c in range(chunks):
-        w_copies[c].wait()
         product = jnp.dot(
             attention, w_buf[:, c * width : (c + 1) * width], preferred_element_type=jnp.float32
         )

time: 28.6 us -> 23.6 us (0.83)
  Pallas kernels: 27 us -> 22 us
    pallas_call x1, Pallas kernels: 27 us -> 22 us  [local(): pl.pallas_call(functools.partial(kernel, seq_size, tensor_size, heads, ch...]
where the time goes in v2:
time: 23.6 us; the launch traced here: 23.4 us
  Pallas kernels  22 us (93%)
  local copies, waits for them, and re-layouts  1.32 us (6%)
    pallas_call x1, Pallas kernels, local(): pl.pallas_call(functools.partial(kernel, seq_size, tensor_size, heads, ch...  22 us
    unnamed x1, local copies, waits for them, and re-layouts  1.32 us

profile of v2, /device:TPU:0, one launch (start us, length us, event | category | flops | bytes accessed | tf_op | source)
XLA Modules:
  0.0 23.4 jit_solution(6757588327109464457)
XLA Ops:
  0.0 22.0 %shard_map.82 = bf16[2,3584]{1,0:T(2,128)(2,1)} custom-call(s32[4]{0:T(128)} %block_seq.1, s32[4]{0:T(128)} %block_pos.1, s32[8]{0:T(128)} %lengths.1, f32[14]{0:T(128)} %slopes.1, bf16[2,1792]{1,0:T(2,128)(2,1)} %query.1, bf16[4,256,1792]{2,1,0:T(8,128)(2,1)} %keys.1, bf16[4,256,1792]{2,1,0:T(8,128)(2,1)} %values.1, bf16[1792,3584]{1,0:T(8,128)(2,1)} %weight.1), custom_call_target="tpu_custom_call" | custom-call | tf_op jit(solution)/shard_map/pallas_call | solution.py:218
  22.0 1.3 %copy.10 = bf16[2,3584]{1,0:T(2,128)(2,1)} copy(bf16[2,3584]{1,0:T(2,128)(2,1)} %shard_map.82) | data formatting | bytes 28672

commit v3 on v2

v3 whole, which is shorter than its diff:
```python
import functools
import math

import jax
import jax.numpy as jnp
from jax import lax
from jax.experimental import pallas as pl
from jax.experimental.pallas import tpu as pltpu
from jax.sharding import PartitionSpec as P

LANES = 128
OWNER_LANE = LANES - 1


def kernel(
    seq_size, tensor_size, groups, chunks,
    block_seq_in, block_pos_in, lengths_in, slopes_in, query, keys, values, weight,
    out,
    block_seq, block_pos, lengths, slopes,
    q_all, k_buf, v_buf, w_buf, stats, accs, held, part, landed,
    small_sem, q_sem, k_sem, v_sem, w_sem,
    q_send, q_recv, s_send, s_recv, a_send, a_recv, p_send, p_recv,
):
    me = lax.axis_index("seq")
    my_rows = lax.axis_index("tensor")
    blocks, block_len, features = k_buf.shape
    heads = slopes.shape[0]
    size = features // heads
    seqs = lengths.shape[0]
    query_rows = q_all.shape[1]
    rows, width = part.shape[2:]
    scale = 1.0 / math.sqrt(size)

    barrier = pltpu.get_barrier_semaphore()
    for k in range(1, seq_size):
        pl.semaphore_signal(barrier, inc=1, device_id={"seq": lax.rem(me + k, seq_size)})
    for k in range(1, tensor_size):
        pl.semaphore_signal(
            barrier, inc=1, device_id={"tensor": lax.rem(my_rows + k, tensor_size)}
        )
    q_copy = pltpu.make_async_copy(query, q_all.at[me], q_sem)
    q_copy.start()
    small_copies = [
        pltpu.make_async_copy(source, target, small_sem.at[i])
        for i, (source, target) in enumerate(
            [
                (block_seq_in, block_seq),
                (block_pos_in, block_pos),
                (lengths_in, lengths),
                (slopes_in, slopes),
            ]
        )
    ]
    for copy in small_copies:
        copy.start()
    cache_copies = [
        pltpu.make_async_copy(cache.at[b], buffer.at[b], sem.at[b])
        for cache, buffer, sem in ((keys, k_buf, k_sem), (values, v_buf, v_sem))
        for b in range(blocks)
    ]
    spans = [(first * size, last * size) for first, last in groups]
    w_copies = [
        pltpu.make_async_copy(
            weight.at[pl.ds(low, high - low)], w_buf.at[pl.ds(low, high - low)], w_sem.at[g]
        )
        for g, (low, high) in enumerate(spans)
    ]

    q_copy.wait()
    for copy in cache_copies:
        copy.start()
    pl.semaphore_wait(barrier, seq_size + tensor_size - 2)

    def to_seq(buffer, send, recv):
        copies = [
            pltpu.make_async_remote_copy(
                src_ref=buffer.at[me],
                dst_ref=buffer.at[me],
                send_sem=send.at[k - 1],
                recv_sem=recv.at[k - 1],
                device_id={"seq": lax.rem(me + k, seq_size)},
            )
            for k in range(1, seq_size)
        ]
        for copy in copies:
            copy.start()
        return copies

    q_sends = to_seq(q_all, q_send, q_recv)

    for copy in small_copies:
        copy.wait()
    offsets = lax.broadcasted_iota(jnp.int32, (1, block_len), 1)
    stat_lane = lax.broadcasted_iota(jnp.int32, (1, LANES), 1)

    for copy in q_sends:
        copy.wait_recv()
    for copy in w_copies:
        copy.start()
    for copy in cache_copies:
        copy.wait()

    q_rows = []
    for b in range(blocks):
        owner = block_seq[b]
        near = q_all[lax.div(owner, query_rows)].astype(jnp.float32)
        which = lax.rem(owner, query_rows)
        q_row = near[:1]
        for r in range(1, query_rows):
            q_row = jnp.where(which == r, near[r : r + 1], q_row)
        q_rows.append(q_row)

    s_sends, a_sends = [], []
    for g, (first, last) in enumerate(groups):
        low, high = spans[g]
        padded = -(-(last - first) // 16) * 16
        lane = lax.broadcasted_iota(jnp.int32, (padded, high - low), 1)
        row = lax.broadcasted_iota(jnp.int32, (padded, high - low), 0)
        of_head = (lane >= row * size) & (lane < row * size + size)
        head_row = lax.broadcasted_iota(jnp.int32, (padded, LANES), 0)
        head_lane = lax.broadcasted_iota(jnp.int32, (padded, LANES), 1)
        slope = jnp.zeros((padded, LANES), jnp.float32)
        for h in range(first, last):
            slope = jnp.where(head_row == h - first, slopes[h], slope)
        slope = slope[:, :1]
        weights, inverse, stat_rows = [], [], []
        for b in range(blocks):
            owner = block_seq[b]
            length = lengths[owner]
            spread = jnp.where(of_head, q_rows[b][:, low:high], 0.0).astype(jnp.bfloat16)
            scores = lax.dot_general(
                spread,
                k_buf[b, :, low:high],
                (((1,), (1,)), ((), ())),
                preferred_element_type=jnp.float32,
            )
            placed = block_pos[b] * block_len + offsets
            live = placed < length
            distance = (length - 1 - placed).astype(jnp.float32)
            scores = jnp.where(live, scores * scale - slope * distance, -1e30)
            top = jnp.max(scores, axis=1, keepdims=True)
            weight_b = jnp.where(live, jnp.exp(scores - top), 0.0)
            total = jnp.sum(weight_b, axis=1, keepdims=True)
            weights.append(weight_b.astype(jnp.bfloat16))
            inverse.append(1.0 / total)
            stat = jnp.sum(
                jnp.where(head_row == head_lane, top + jnp.log(total), 0.0), axis=0, keepdims=True
            )
            stat_rows.append(jnp.where(stat_lane == OWNER_LANE, owner.astype(jnp.float32), stat))
        stats[g][me] = jnp.concatenate(stat_rows, axis=0)
        s_sends.append(to_seq(stats[g], s_send.at[g], s_recv.at[g]))
        acc_rows = []
        for b in range(blocks):
            summed = jnp.dot(
                weights[b], v_buf[b, :, low:high], preferred_element_type=jnp.float32
            )
            summed = summed * inverse[b]
            acc_rows.append(jnp.sum(jnp.where(of_head, summed, 0.0), axis=0, keepdims=True))
        accs[g][me] = jnp.concatenate(acc_rows, axis=0).astype(jnp.bfloat16)
        a_sends.append(to_seq(accs[g], a_send.at[g], a_recv.at[g]))

    def attention_of(g):
        for copy in s_sends[g]:
            copy.wait_recv()
        stat = stats[g][...]
        owners = stat[:, :, OWNER_LANE:]
        best = jnp.zeros_like(stat)
        masks = [owners == float(s) for s in range(seqs)]
        for s in range(seqs):
            top = jnp.max(jnp.where(masks[s], stat, -1e30), axis=(0, 1), keepdims=True)
            best = jnp.where(masks[s], top, best)
        grown = jnp.exp(stat - best)
        whole = jnp.ones_like(stat)
        for s in range(seqs):
            total = jnp.sum(jnp.where(masks[s], grown, 0.0), axis=(0, 1), keepdims=True)
            whole = jnp.where(masks[s], total, whole)
        factor = grown / whole
        seq_lane = lax.broadcasted_iota(jnp.int32, (blocks, LANES), 1).astype(jnp.float32)
        owned = jnp.concatenate(
            [jnp.where(owners[j] == seq_lane, 1.0, 0.0) for j in range(seq_size)], axis=0
        )
        owned = owned.T[:seqs].astype(jnp.bfloat16)
        first, last = groups[g]
        spread = [
            jnp.concatenate(
                [
                    jnp.broadcast_to(factor[j][:, h : h + 1], (blocks, size))
                    for h in range(last - first)
                ],
                axis=1,
            )
            for j in range(seq_size)
        ]
        for copy in a_sends[g]:
            copy.wait_recv()
        w_copies[g].wait()
        scaled = jnp.concatenate(
            [accs[g][j].astype(jnp.float32) * spread[j] for j in range(seq_size)], axis=0
        )
        upper = scaled.astype(jnp.bfloat16)
        lower = (scaled - upper.astype(jnp.float32)).astype(jnp.bfloat16)
        attention = jnp.dot(owned, upper, preferred_element_type=jnp.float32) + jnp.dot(
            owned, lower, preferred_element_type=jnp.float32
        )
        return attention.astype(jnp.bfloat16)

    for g, (low, high) in enumerate(spans[:-1]):
        attention = attention_of(g)
        product = jnp.dot(attention, w_buf[low:high], preferred_element_type=jnp.float32)
        held[...] = product if g == 0 else held[...] + product
    attention = attention_of(len(groups) - 1)
    low, high = spans[-1]

    p_sends = []
    for c in range(chunks):
        columns = slice(c * width, (c + 1) * width)
        product = jnp.dot(attention, w_buf[low:high, columns], preferred_element_type=jnp.float32)
        product = product + held[:, columns]
        for r in range(tensor_size):
            part[r, c] = product[r * rows : (r + 1) * rows]
        sends = []
        for k in range(1, tensor_size):
            peer = lax.rem(my_rows + k, tensor_size)
            copy = pltpu.make_async_remote_copy(
                src_ref=part.at[peer, c],
                dst_ref=landed.at[k - 1, c],
                send_sem=p_send.at[k - 1, c],
                recv_sem=p_recv.at[k - 1, c],
                device_id={"tensor": peer},
            )
            copy.start()
            sends.append(copy)
        p_sends.append(sends)
    for c in range(chunks):
        total = part[my_rows, c]
        for k in range(1, tensor_size):
            p_sends[c][k - 1].wait_recv()
            total = total + landed[k - 1, c]
        out[:, c * width : (c + 1) * width] = total.astype(out.dtype)
    for sends in [q_sends] + s_sends + a_sends + p_sends:
        for copy in sends:
            copy.wait_send()


def local(seq_size, tensor_size, query, key_cache, value_cache, slopes, block_seq, block_pos, lengths, weight):
    heads = slopes.shape[0]
    blocks, block_len, features = key_cache.shape
    size = features // heads
    columns = weight.shape[1]
    chunks = max([c for c in range(1, 9) if columns % (c * 256) == 0], default=1)
    width = columns // chunks
    rows = lengths.shape[0] // tensor_size
    middle = min(heads, -(-heads // 4) * 2)
    groups = [(low, high) for low, high in ((0, middle), (middle, heads)) if high > low]
    smalls = (block_seq, block_pos, lengths, slopes)
    dma = pltpu.SemaphoreType.DMA
    return pl.pallas_call(
        functools.partial(kernel, seq_size, tensor_size, groups, chunks),
        out_shape=pltpu.VMEM((rows, columns), jnp.bfloat16),
        in_specs=[pl.BlockSpec(memory_space=pltpu.HBM)] * 8,
        out_specs=pl.BlockSpec(memory_space=pltpu.VMEM),
        scratch_shapes=[pltpu.SMEM(a.shape, a.dtype) for a in smalls]
        + [
            pltpu.VMEM((seq_size,) + query.shape, query.dtype),
            pltpu.VMEM(key_cache.shape, key_cache.dtype),
            pltpu.VMEM(value_cache.shape, value_cache.dtype),
            pltpu.VMEM(weight.shape, weight.dtype),
            [pltpu.VMEM((seq_size, blocks, LANES), jnp.float32) for _ in groups],
            [
                pltpu.VMEM((seq_size, blocks, (high - low) * size), jnp.bfloat16)
                for low, high in groups
            ],
            pltpu.VMEM((lengths.shape[0], columns), jnp.float32),
            pltpu.VMEM((tensor_size, chunks, rows, width), jnp.float32),
            pltpu.VMEM((tensor_size - 1, chunks, rows, width), jnp.float32),
            dma((4,)),
            dma,
            dma((blocks,)),
            dma((blocks,)),
            dma((len(groups),)),
        ]
        + [dma((seq_size - 1,))] * 2
        + [dma((len(groups), seq_size - 1))] * 4
        + [dma((tensor_size - 1, chunks))] * 2,
        compiler_params=pltpu.CompilerParams(
            collective_id=0, has_side_effects=True, vmem_limit_bytes=48 * 1024 * 1024
        ),
    )(
        *[
            pltpu.with_memory_space_constraint(a, pltpu.HBM)
            for a in smalls + (query, key_cache, value_cache, weight)
        ]
    )


def solution(mesh):
    placed = (
        P(("group", "seq"), "tensor"),
        P(("group", "seq"), None, "tensor"),
        P(("group", "seq"), None, "tensor"),
        P("tensor"),
        P(("group", "seq")),
        P(("group", "seq")),
        P("group"),
        P("tensor", "seq"),
    )
    return jax.shard_map(
        functools.partial(local, mesh.shape["seq"], mesh.shape["tensor"]),
        mesh=mesh,
        in_specs=placed,
        out_specs=P(("group", "tensor"), "seq"),
        check_vma=False,
    )
```

time: 23.6 us -> 21.2 us (0.90)
  Pallas kernels: 22 us -> 20.5 us
  local copies, waits for them, and re-layouts: 1.32 us -> 0.6 us
    pallas_call x1, Pallas kernels: 22 us -> 20.5 us  [local(): pl.pallas_call(functools.partial(kernel, seq_size, tensor_size, groups, c...]
    unnamed x1, local copies, waits for them, and re-layouts: 1.32 us -> 0.6 us
where the time goes in v3:
time: 21.2 us; the launch traced here: 21.1 us
  Pallas kernels  20.5 us (97%)
  local copies, waits for them, and re-layouts  0.6 us (3%)
    pallas_call x1, Pallas kernels, local(): pl.pallas_call(functools.partial(kernel, seq_size, tensor_size, groups, c...  20.5 us
    unnamed x1, local copies, waits for them, and re-layouts  0.6 us

profile of v3, /device:TPU:0, one launch (start us, length us, event | category | flops | bytes accessed | tf_op | source)
XLA Modules:
  0.0 21.1 jit_solution(4671693596295874586)
XLA Ops:
  0.0 20.5 %shard_map.82 = bf16[2,3584]{1,0:T(2,128)(2,1)S(1)} custom-call(s32[4]{0:T(128)} %block_seq_in.1, s32[4]{0:T(128)} %block_pos_in.1, s32[8]{0:T(128)} %lengths_in.1, f32[14]{0:T(128)} %slopes_in.1, bf16[2,1792]{1,0:T(2,128)(2,1)} %query.1, bf16[4,256,1792]{2,1,0:T(8,128)(2,1)} %keys.1, bf16[4,256,1792]{2,1,0:T(8,128)(2,1)} %values.1, bf16[1792,3584]{1,0:T(8,128)(2,1)} %weight.1), custom_call_target="tpu_custom_call" | custom-call | tf_op jit(solution)/shard_map/pallas_call | solution.py:257
  20.5 0.6 %copy.10 = bf16[2,3584]{1,0:T(2,128)(2,1)} copy(bf16[2,3584]{1,0:T(2,128)(2,1)S(1)} %shard_map.82) | data formatting | bytes 28672

commit v4 on v3

--- a/solution.py
+++ b/solution.py
@@ -212,10 +212,17 @@
     low, high = spans[-1]
 
     p_sends = []
-    for c in range(chunks):
+
+    def product_of(c):
         columns = slice(c * width, (c + 1) * width)
         product = jnp.dot(attention, w_buf[low:high, columns], preferred_element_type=jnp.float32)
-        product = product + held[:, columns]
+        return product + held[:, columns]
+
+    later = product_of(0)
+    for c in range(chunks):
+        product = later
+        if c + 1 < chunks:
+            later = product_of(c + 1)
         for r in range(tensor_size):
             part[r, c] = product[r * rows : (r + 1) * rows]
         sends = []

time: 21.2 us -> 20.6 us (0.972)
  Pallas kernels: 20.5 us -> 19.8 us
    pallas_call x1, Pallas kernels: 20.5 us -> 19.8 us  [local(): pl.pallas_call(functools.partial(kernel, seq_size, tensor_size, groups, c...]
where the time goes in v4:
time: 20.6 us; the launch traced here: 20.5 us
  Pallas kernels  19.8 us (96%)
  local copies, waits for them, and re-layouts  0.6 us (3%)
    pallas_call x1, Pallas kernels, local(): pl.pallas_call(functools.partial(kernel, seq_size, tensor_size, groups, c...  19.8 us
    unnamed x1, local copies, waits for them, and re-layouts  0.6 us

profile of v4, /device:TPU:0, one launch (start us, length us, event | category | flops | bytes accessed | tf_op | source)
XLA Modules:
  0.0 20.5 jit_solution(7092304392621512264)
XLA Ops:
  0.0 19.8 %shard_map.82 = bf16[2,3584]{1,0:T(2,128)(2,1)S(1)} custom-call(s32[4]{0:T(128)} %block_seq_in.1, s32[4]{0:T(128)} %block_pos_in.1, s32[8]{0:T(128)} %lengths_in.1, f32[14]{0:T(128)} %slopes_in.1, bf16[2,1792]{1,0:T(2,128)(2,1)} %query.1, bf16[4,256,1792]{2,1,0:T(8,128)(2,1)} %keys.1, bf16[4,256,1792]{2,1,0:T(8,128)(2,1)} %values.1, bf16[1792,3584]{1,0:T(8,128)(2,1)} %weight.1), custom_call_target="tpu_custom_call" | custom-call | tf_op jit(solution)/shard_map/pallas_call | solution.py:264
  19.9 0.6 %copy.10 = bf16[2,3584]{1,0:T(2,128)(2,1)} copy(bf16[2,3584]{1,0:T(2,128)(2,1)S(1)} %shard_map.82) | data formatting | bytes 28672
